TPU v7x, 512 devices: a whole 4x8x8 slice. The times are simulated.
512 devices in a mesh: space: 64 (over y_lo, z, x), tensor: 8 (over y_hi, core).
Axes of the slice: x: 4, y: 8 (y_hi: 4, y_lo: 2; y = y_hi * 2 + y_lo), z: 8, core: 2. Of those that a mesh axis runs over, the one named last changes fastest.
Arguments:
- tokens: float32 [2, 128, 128, 2048], P(None, 'space', None, 'tensor'), may hold values from -6 to 6
- in_gain: float32 [2048], replicated, may hold values from 0.25 to 1.75
- w_inner: bfloat16 [2048, 3072], P(None, 'tensor'), may hold values from -0.125 to 0.125
- w_bc: bfloat16 [2048, 256], replicated, may hold values from -0.03125 to 0.03125
- w_step: bfloat16 [2048, 48], P(None, 'tensor'), may hold values from -0.125 to 0.125
- step_bias: float32 [48], P('tensor'), may hold values from -3 to 0
- decay_rate: float32 [48], P('tensor'), may hold values from 0.02 to 2
- skip: float32 [48], P('tensor'), may hold values from 0.5 to 2
- norm_gain: float32 [3072], P('tensor'), may hold values from 0.25 to 1.75
- w_out: bfloat16 [3072, 2048], P('tensor'), may hold values from -0.109375 to 0.109375
Outputs:
- mixed: bfloat16 [2, 128, 128, 2048], P(None, 'space', None, 'tensor')
All inputs are finite; a program needn't handle non-finite values.
Results may differ from a plain program's by a relative error of at most 0.011.
Values may be sent and summed in bfloat16 or wider, within the bound.
No kernel may reach another device: no remote copies, remote signals or barrier semaphores. Data moves between devices by JAX's collectives and lax.ppermute only.
A program may use at most 64 MiB of HBM per device.

v0:
```python
import jax
import jax.numpy as jnp
from jax import lax
from jax.sharding import PartitionSpec as P

HEAD_DIM = 64
STATE = 128
NORM_HEADS = 6
EPS = 1e-05


def kernel(logdecay):
    running = jnp.cumsum(logdecay, axis=-1)
    length = logdecay.shape[-1]
    place = jnp.arange(length)
    lower = place[:, None] >= place[None, :]
    upper = place[:, None] <= place[None, :]
    later = running[..., :, None] - running[..., None, :]
    shifted = running - logdecay
    earlier = shifted[..., None, :] - shifted[..., :, None]
    forward = jnp.exp(jnp.where(lower, later, -jnp.inf))
    backward = jnp.exp(jnp.where(upper, earlier, -jnp.inf))
    return forward + backward


def scan_grid(values, maps, logdecay, along_rows):
    heads = logdecay.shape[-1]
    in_map = maps[..., :STATE]
    out_map = maps[..., STATE:]
    split_values = values.reshape(values.shape[:3] + (heads, HEAD_DIM))
    if along_rows:
        scores = jnp.einsum("ialn,iamn->ialm", out_map, in_map, preferred_element_type=jnp.float32)
        decays = jnp.moveaxis(logdecay.astype(jnp.float32), 3, 2)
    else:
        scores = jnp.einsum("ilan,iman->ialm", out_map, in_map, preferred_element_type=jnp.float32)
        decays = jnp.transpose(logdecay.astype(jnp.float32), (0, 2, 3, 1))
    weights = (scores[:, :, None] * kernel(decays)).astype(jnp.bfloat16)
    if along_rows:
        result = jnp.einsum(
            "iahlm,iamhp->ialhp", weights, split_values, preferred_element_type=jnp.float32
        )
    else:
        result = jnp.einsum(
            "iahlm,imahp->ilahp", weights, split_values, preferred_element_type=jnp.float32
        )
    return result.reshape(values.shape)


def on_device(
    tokens, in_gain, w_inner, w_bc, w_step, step_bias, decay_rate, skip, norm_gain, w_out
):
    whole = lax.all_gather(tokens.astype(jnp.bfloat16), "tensor", axis=3, tiled=True)
    rounded = whole.astype(jnp.float32)
    scale = lax.rsqrt(jnp.mean(rounded * rounded, axis=-1, keepdims=True) + EPS)
    normed = (rounded * scale * in_gain).astype(jnp.bfloat16)
    inner = jnp.einsum("irwd,dc->irwc", normed, w_inner, preferred_element_type=jnp.float32).astype(
        jnp.bfloat16
    )
    maps = jnp.einsum("irwd,dc->irwc", normed, w_bc, preferred_element_type=jnp.float32).astype(
        jnp.bfloat16
    )
    step = jax.nn.softplus(
        jnp.einsum("irwd,dc->irwc", normed, w_step, preferred_element_type=jnp.float32) + step_bias
    )
    logdecay = (-decay_rate * step).astype(jnp.bfloat16)
    heads_local = w_step.shape[1]
    lead = inner.shape[:3]
    value = (
        (inner.reshape(lead + (heads_local, HEAD_DIM)).astype(jnp.float32) * step[..., None])
        .reshape(inner.shape)
        .astype(jnp.bfloat16)
    )
    col_value = lax.all_to_all(value, "space", split_axis=2, concat_axis=1, tiled=True)
    col_maps = lax.all_to_all(maps, "space", split_axis=2, concat_axis=1, tiled=True)
    col_decay = lax.all_to_all(logdecay, "space", split_axis=2, concat_axis=1, tiled=True)
    column_out = scan_grid(col_value, col_maps, col_decay, False).astype(jnp.bfloat16)
    column_back = lax.all_to_all(column_out, "space", split_axis=1, concat_axis=2, tiled=True)
    row_out = scan_grid(value, maps, logdecay, True)
    skip_wide = jnp.repeat(skip, HEAD_DIM)
    total = row_out + column_back.astype(jnp.float32) + skip_wide * inner.astype(jnp.float32)
    group = NORM_HEADS * HEAD_DIM
    grouped = total.reshape(lead + (inner.shape[3] // group, group))
    norm_scale = lax.rsqrt(jnp.mean(grouped * grouped, axis=-1, keepdims=True) + EPS)
    gated = ((grouped * norm_scale).reshape(inner.shape) * norm_gain).astype(jnp.bfloat16)
    partial_out = jnp.einsum("irwc,cd->irwd", gated, w_out, preferred_element_type=jnp.float32)
    mixer = lax.psum_scatter(partial_out, "tensor", scatter_dimension=3, tiled=True)
    return (tokens + mixer).astype(jnp.bfloat16)


def solution(mesh):
    return jax.shard_map(
        on_device,
        mesh=mesh,
        in_specs=(
            P(None, "space", None, "tensor"),
            P(),
            P(None, "tensor"),
            P(),
            P(None, "tensor"),
            P("tensor"),
            P("tensor"),
            P("tensor"),
            P("tensor"),
            P("tensor", None),
        ),
        out_specs=P(None, "space", None, "tensor"),
        check_vma=False,
    )
```

profile of v0, /device:TPU:19, one launch (start us, length us, event | category | flops | bytes accessed | tf_op | source)
XLA Modules:
  0.0 218.5 jit_solution(5063790395113188788)
XLA Ops:
  6.6 1.9 convert_element_type.76
  8.5 0.7 neg.11
  9.2 45.6 %all-gather.2.cloned.1.call-done = bf16[2,2,128,2048]{3,2,1,0:T(8,128)(2,1)} async-done(((bf16[2,2,128,256]{3,2,1,0:T(8,128)(2,1)}), bf16[2,2,128,2048]{3,2,1,0:T(8,128)(2,1)}) %all-gather.2.cloned.1.call-update) | async-done | bytes 2097168 | tf_op jit(solution)/shard_map/all_gather | solution.py:52
  54.7 2.2 %fusion = f32[2,2,128]{2,1,0:T(2,128)S(1)} fusion(bf16[2,2,128,2048]{3,2,1,0:T(8,128)(2,1)} %all-gather.2.cloned.1.call-done), kind=kLoop, calls=%fused_computation.2 | loop fusion | flops 3145216 | bytes 2099200 | tf_op jit(solution)/shard_map/reduce_sum | solution.py:54
  57.0 0.8 multiply_convert_fusion.7
  57.8 0.8 copy.52
  58.6 12.8 %all-to-all-start.2 = ((bf16[2,2,128,6]{3,1,0,2:T(2,128)(2,1)}), bf16[2,2,128,6]{3,1,0,2:T(2,128)(2,1)S(1)}, u32[]{:S(2)}, u32[]{:S(2)}) async-start(bf16[2,2,128,6]{3,1,0,2:T(2,128)(2,1)} %copy.52), calls=%async_computation.2 | async-start | bytes 262144 | tf_op jit(solution)/shard_map/all_to_all | solution.py:75
  71.5 2.4 %convolution_convert_fusion.1 = bf16[2,2,128,256]{3,2,1,0:T(8,128)(2,1)S(1)} fusion(bf16[2,2,128,2048]{3,2,1,0:T(8,128)(2,1)} %all-gather.2.cloned.1.call-done, f32[2048]{0:T(1024)S(1)} %copy-done.13, f32[2,2,128]{2,1,0:T(2,128)S(1)} %add_rsqrt_fusion.1, bf16[2048,256]{1,0:T(8,128)(2,1)S(1)} %copy-done.11), kind=kOutput, calls=%fused_computation.14 | convolution fusion | flops 541196288 | bytes 3418112 | tf_op jit(solution)/shard_map/irwd,dc->irwc/dot_general | solution.py:59
  73.8 1.0 copy.48
  74.8 5.6 %all-to-all-done.2 = bf16[2,2,128,6]{3,1,0,2:T(2,128)(2,1)S(1)} async-done(((bf16[2,2,128,6]{3,1,0,2:T(2,128)(2,1)}), bf16[2,2,128,6]{3,1,0,2:T(2,128)(2,1)S(1)}, u32[]{:S(2)}, u32[]{:S(2)}) %all-to-all-start.2) | async-done | bytes 6176 | tf_op jit(solution)/shard_map/all_to_all | solution.py:75
  80.5 6.1 %all-to-all-start.1 = ((bf16[2,2,128,256]{3,1,0,2:T(2,128)(2,1)}), bf16[2,2,128,256]{3,1,0,2:T(2,128)(2,1)S(1)}, u32[]{:S(2)}, u32[]{:S(2)}) async-start(bf16[2,2,128,256]{3,1,0,2:T(2,128)(2,1)} %copy.48), calls=%async_computation.1 | async-start | bytes 524288 | tf_op jit(solution)/shard_map/all_to_all | solution.py:74
  86.6 0.1 broadcast_in_dim.25
  86.6 0.7 mul.106
  87.4 1.2 copy.44
  88.5 4.4 %multiply_convert_fusion.5 = (bf16[2,2,128,384]{3,2,1,0:T(8,128)(2,1)S(1)}, f32[2,2,128,384]{3,2,1,0:T(8,128)}) fusion(f32[2,2,128,384]{3,2,1,0:T(8,128)} %copy.44, bf16[2048,384]{1,0:T(8,128)(2,1)} %param.12, bf16[2,2,128,2048]{3,2,1,0:T(8,128)(2,1)} %all-gather.2.cloned.1.call-done, f32[2048]{0:T(1024)S(1)} %copy-done.13, ...), kind=kOutput, calls=%fused_computation.34 | convolution fusion | flops 810287104 | bytes 5646336 | tf_op jit(solution)/shard_map/irwd,dc->irwc/dot_general | solution.py:56
  92.9 1.1 copy.46
  94.1 2.0 all-to-all-done.1
  96.1 8.8 %all-to-all-start = ((bf16[2,2,128,384]{3,1,0,2:T(2,128)(2,1)}), bf16[2,2,128,384]{3,1,0,2:T(2,128)(2,1)S(1)}, u32[]{:S(2)}, u32[]{:S(2)}) async-start(bf16[2,2,128,384]{3,1,0,2:T(2,128)(2,1)} %copy.46), calls=%async_computation | async-start | bytes 786432 | tf_op jit(solution)/shard_map/all_to_all | solution.py:73
  104.8 0.6 iota_compare_fusion
  105.5 0.1 copy.53
  105.6 0.2 copy.54
  105.7 0.2 copy.55
  105.9 0.1 copy.56
  106.1 1.1 reduce_window_sum.18
  107.2 0.6 bitcast_subtract_fusion
  107.8 0.2 copy.49
  108.0 0.2 fusion.53
  108.2 0.2 fusion.40
  108.4 6.6 %all-to-all-done = bf16[2,2,128,384]{3,1,0,2:T(2,128)(2,1)S(1)} async-done(((bf16[2,2,128,384]{3,1,0,2:T(2,128)(2,1)}), bf16[2,2,128,384]{3,1,0,2:T(2,128)(2,1)S(1)}, u32[]{:S(2)}, u32[]{:S(2)}) %all-to-all-start) | async-done | bytes 393248 | tf_op jit(solution)/shard_map/all_to_all | solution.py:73
  115.0 0.3 copy.77
  115.3 1.6 reshape.67
  116.9 2.5 %convolution_convert_fusion = bf16[2,2,6,64,128]{4,3,2,1,0:T(8,128)(2,1)S(1)} fusion(bf16[2,128,2,6,64]{4,3,2,1,0:T(8,128)(2,1)} %reshape.67, f32[2,2,6,128]{3,2,1,0:T(8,128)} %bitcast_subtract_fusion, f32[2,2,6,128]{3,2,1,0:T(8,128)} %copy-done.3, f32[2,2,128,128]{3,2,1,0:T(8,128)S(1)} %fusion.40, pred[128,128]{1,0:T(8,128)(4,1)} %get-tuple-element.14, ...), kind=kOutput, calls=%fused_computation.13 | convolution fusion | flops 53280768 | bytes 1105920 | tf_op jit(solution)/shard_map/iahlm,imahp->ilahp/dot_general | solution.py:43
  119.4 1.1 copy.58
  120.5 10.5 %all-to-all-start.3 = ((bf16[2,128,2,384]{3,2,0,1:T(2,128)(2,1)}), bf16[2,128,2,384]{3,2,0,1:T(2,128)(2,1)S(1)}, u32[]{:S(2)}, u32[]{:S(2)}) async-start(bf16[2,128,2,384]{3,2,0,1:T(2,128)(2,1)} %copy.58), calls=%async_computation.3 | async-start | bytes 786432 | tf_op jit(solution)/shard_map/all_to_all | solution.py:77
  131.0 0.2 reduce-scatter.2.cloned.1.call-start
  131.3 0.2 copy.45
  131.6 1.2 reduce_window_sum.17
  132.8 0.2 fusion.37
  133.0 2.0 fusion.17
  135.1 1.4 copy.62
  136.5 4.8 %all-to-all-done.3 = bf16[2,128,2,384]{3,2,0,1:T(2,128)(2,1)S(1)} async-done(((bf16[2,128,2,384]{3,2,0,1:T(2,128)(2,1)}), bf16[2,128,2,384]{3,2,0,1:T(2,128)(2,1)S(1)}, u32[]{:S(2)}, u32[]{:S(2)}) %all-to-all-start.3) | async-done | bytes 393248 | tf_op jit(solution)/shard_map/all_to_all | solution.py:77
  141.3 0.6 copy.60
  142.0 0.3 copy.61
  142.2 1.4 reshape.68
  143.7 1.6 multiply_reduce_fusion
  145.3 3.3 %fusion.3 = f32[2,2,128,2048]{3,2,1,0:T(8,128)} fusion(bf16[384,2048]{1,0:T(8,128)(2,1)S(1)} %copy-done, f32[2,2,128,384]{3,2,1,0:T(8,128)S(1)} %get-tuple-element.6, f32[384]{0:T(512)S(1)} %copy-done.7, f32[2,2,128]{2,1,0:T(2,128)S(1)} %add_rsqrt_fusion), kind=kOutput, calls=%fused_computation.5 | convolution fusion | flops 805896192 | bytes 6557184 | tf_op jit(solution)/shard_map/irwc,cd->irwd/dot_general | solution.py:85
  148.6 61.3 %reduce-scatter.2.cloned.1.call-done = f32[2,2,128,256]{3,2,1,0:T(8,128)} async-done(((f32[2,2,128,2048]{3,2,1,0:T(8,128)}), f32[2,2,128,256]{3,2,1,0:T(8,128)}) %reduce-scatter.2.cloned.1.call-update) | async-done | bytes 524304 | tf_op jit(solution)/shard_map/reduce_scatter | solution.py:86
  209.8 1.8 add_convert_fusion
  (39 shorter events, 0.4 us)
Async XLA Ops:
  6.5 138.7 %copy-start = (bf16[384,2048]{1,0:T(8,128)(2,1)S(1)}, bf16[384,2048]{1,0:T(8,128)(2,1)}, u32[]{:S(2)}) copy-start(bf16[384,2048]{1,0:T(8,128)(2,1)} %param.19) | copy-start | bytes 4718596
  6.5 50.4 %copy-start.13 = (f32[2048]{0:T(1024)S(1)}, f32[2048]{0:T(1024)}, u32[]{:S(2)}) copy-start(f32[2048]{0:T(1024)} %param.11) | copy-start | bytes 24580
  6.5 50.4 %copy-start.14 = (f32[6]{0:T(128)S(1)}, f32[6]{0:T(128)}, u32[]{:S(2)}) copy-start(f32[6]{0:T(128)} %param.15) | copy-start | bytes 76
  6.5 50.5 %copy-start.12 = (bf16[2048,6]{0,1:T(8,128)(2,1)S(1)}, bf16[2048,6]{0,1:T(8,128)(2,1)}, u32[]{:S(2)}) copy-start(bf16[2048,6]{0,1:T(8,128)(2,1)} %param.14) | copy-start | bytes 73732
  6.5 48.2 %all-gather.2.cloned.1.call-start = ((), (), s32[]{:S(2)}) async-start(), calls=%async_computation.5 | async-start | bytes 2359296 | tf_op jit(solution)/shard_map/all_gather | solution.py:52
  9.2 48.7 %copy-start.8 = (f32[6]{0:T(128)}, f32[6]{0:T(128)S(1)}, u32[]{:S(2)}) copy-start(f32[6]{0:T(128)S(1)} %neg.11) | copy-start | bytes 76
  54.7 2.3 %copy-start.1 = (bf16[2,2,128,2048]{3,2,1,0:T(8,128)(2,1)S(1)}, bf16[2,2,128,2048]{3,2,1,0:T(8,128)(2,1)}, u32[]{:S(2)}) copy-start(bf16[2,2,128,2048]{3,2,1,0:T(8,128)(2,1)} %all-gather.2.cloned.1.call-done) | copy-start | bytes 6291460
  57.0 14.4 %copy-start.11 = (bf16[2048,256]{1,0:T(8,128)(2,1)S(1)}, bf16[2048,256]{1,0:T(8,128)(2,1)}, u32[]{:S(2)}) copy-start(bf16[2048,256]{1,0:T(8,128)(2,1)} %param.13) | copy-start | bytes 3145732
  58.6 21.8 %all-to-all-start.2 = ((bf16[2,2,128,6]{3,1,0,2:T(2,128)(2,1)}), bf16[2,2,128,6]{3,1,0,2:T(2,128)(2,1)S(1)}, u32[]{:S(2)}, u32[]{:S(2)}) async-start(bf16[2,2,128,6]{3,1,0,2:T(2,128)(2,1)} %copy.52), calls=%async_computation.2 | async-start | bytes 262144 | tf_op jit(solution)/shard_map/all_to_all | solution.py:75
  71.5 15.1 %copy-start.10 = (f32[6]{0:T(128)S(1)}, f32[6]{0:T(128)}, u32[]{:S(2)}) copy-start(f32[6]{0:T(128)} %param.17) | copy-start | bytes 76
  80.5 15.6 %all-to-all-start.1 = ((bf16[2,2,128,256]{3,1,0,2:T(2,128)(2,1)}), bf16[2,2,128,256]{3,1,0,2:T(2,128)(2,1)S(1)}, u32[]{:S(2)}, u32[]{:S(2)}) async-start(bf16[2,2,128,256]{3,1,0,2:T(2,128)(2,1)} %copy.48), calls=%async_computation.1 | async-start | bytes 524288 | tf_op jit(solution)/shard_map/all_to_all | solution.py:74
  96.1 18.9 %all-to-all-start = ((bf16[2,2,128,384]{3,1,0,2:T(2,128)(2,1)}), bf16[2,2,128,384]{3,1,0,2:T(2,128)(2,1)S(1)}, u32[]{:S(2)}, u32[]{:S(2)}) async-start(bf16[2,2,128,384]{3,1,0,2:T(2,128)(2,1)} %copy.46), calls=%async_computation | async-start | bytes 786432 | tf_op jit(solution)/shard_map/all_to_all | solution.py:73
  107.2 7.8 %copy-start.3 = (f32[2,2,6,128]{3,2,1,0:T(8,128)}, f32[2,2,6,128]{3,2,1,0:T(8,128)S(1)}, u32[]{:S(2)}) copy-start(f32[2,2,6,128]{3,2,1,0:T(8,128)S(1)} %reduce_window_sum.18) | copy-start | bytes 36868
  119.4 11.9 %copy-start.9 = (f32[6]{0:T(128)S(1)}, f32[6]{0:T(128)}, u32[]{:S(2)}) copy-start(f32[6]{0:T(128)} %copy-done.8) | copy-start | bytes 76
  119.4 13.6 %copy-start.4 = (pred[128,128]{1,0:T(8,128)(4,1)S(1)}, pred[128,128]{1,0:T(8,128)(4,1)}, u32[]{:S(2)}) copy-start(pred[128,128]{1,0:T(8,128)(4,1)} %get-tuple-element.14) | copy-start | bytes 49156
  119.4 13.6 %copy-start.5 = (pred[128,128]{1,0:T(8,128)(4,1)S(1)}, pred[128,128]{1,0:T(8,128)(4,1)}, u32[]{:S(2)}) copy-start(pred[128,128]{1,0:T(8,128)(4,1)} %get-tuple-element.15) | copy-start | bytes 49156
  120.5 20.8 %all-to-all-start.3 = ((bf16[2,128,2,384]{3,2,0,1:T(2,128)(2,1)}), bf16[2,128,2,384]{3,2,0,1:T(2,128)(2,1)S(1)}, u32[]{:S(2)}, u32[]{:S(2)}) async-start(bf16[2,128,2,384]{3,2,0,1:T(2,128)(2,1)} %copy.58), calls=%async_computation.3 | async-start | bytes 786432 | tf_op jit(solution)/shard_map/all_to_all | solution.py:77
  131.0 78.8 %reduce-scatter.2.cloned.1.call-start = ((), (), s32[]{:S(2)}) async-start(), calls=%async_computation.6 | async-start | bytes 4718592 | tf_op jit(solution)/shard_map/reduce_scatter | solution.py:86
  141.9 1.7 copy-start.6
  143.7 1.6 copy-start.7
  148.6 61.3 %copy-start.2 = (f32[2,2,128,256]{3,2,1,0:T(8,128)S(1)}, f32[2,2,128,256]{3,2,1,0:T(8,128)}, u32[]{:S(2)}) copy-start(f32[2,2,128,256]{3,2,1,0:T(8,128)} %param.10) | copy-start | bytes 1572868
Sparse Core Ops, SparseCore 0:
  9.5 45.2 all-gather.1
  148.7 61.0 reduce-scatter.1
where the time goes:
time: 219 us; the launch traced here: 218 us
  waiting for transfers between devices  126 us (58%)
  starting transfers between devices  38.4 us (18%)
  matrix products  15.8 us (7%)
  between operations  13.7 us (6%)
  local copies, waits for them, and re-layouts  12.8 us (6%)
  other arithmetic  11.9 us (5%)
    reduce_scatter x1, waiting for transfers between devices, on_device(): lax.psum_scatter(partial_out, 'tensor', scatter_dimension=3, tiled=True)  61.3 us
    all_gather x1, waiting for transfers between devices, on_device(): lax.all_gather(tokens.astype(jnp.bfloat16), 'tensor', axis=3, tiled=True)  45.6 us
    all_to_all x1, starting transfers between devices, on_device(): lax.all_to_all(logdecay, 'space', split_axis=2, concat_axis=1, tiled=True)  12.8 us
    all_to_all x1, starting transfers between devices, on_device(): lax.all_to_all(column_out, 'space', split_axis=1, concat_axis=2, tiled=True)  10.5 us
    all_to_all x1, starting transfers between devices, on_device(): lax.all_to_all(value, 'space', split_axis=2, concat_axis=1, tiled=True)  8.77 us
    all_to_all x1, waiting for transfers between devices, on_device(): lax.all_to_all(value, 'space', split_axis=2, concat_axis=1, tiled=True)  6.57 us
    all_to_all x1, starting transfers between devices, on_device(): lax.all_to_all(maps, 'space', split_axis=2, concat_axis=1, tiled=True)  6.09 us
    all_to_all x1, waiting for transfers between devices, on_device(): lax.all_to_all(logdecay, 'space', split_axis=2, concat_axis=1, tiled=True)  5.64 us
  transfers between devices with their start and end apart: 6, of which 6 were waited for; matrix products, arithmetic and copies ran while one was open for 9% of the time, Pallas kernels for 0%

commit v1 on v0

--- a/solution.py
+++ b/solution.py
@@ -49,7 +49,12 @@
 def on_device(
     tokens, in_gain, w_inner, w_bc, w_step, step_bias, decay_rate, skip, norm_gain, w_out
 ):
-    whole = lax.all_gather(tokens.astype(jnp.bfloat16), "tensor", axis=3, tiled=True)
+    whole = jnp.concatenate(
+        lax.all_to_all(
+            jnp.stack([tokens.astype(jnp.bfloat16)] * lax.axis_size("tensor")), "tensor", 0, 0
+        ),
+        axis=3,
+    )
     rounded = whole.astype(jnp.float32)
     scale = lax.rsqrt(jnp.mean(rounded * rounded, axis=-1, keepdims=True) + EPS)
     normed = (rounded * scale * in_gain).astype(jnp.bfloat16)

time: 219 us -> 235 us (1.073)
  starting transfers between devices: 38.4 us -> 45.1 us
  local copies, waits for them, and re-layouts: 12.8 us -> 18.6 us
  waiting for transfers between devices: 126 us -> 131 us
    all_to_all x0 -> x1, waiting for transfers between devices: none -> 49.1 us  [on_device(): lax.all_to_all(jnp.stack([tokens.astype(jnp.bfloat16)] * lax.axis_size('t...]
    all_gather x1 -> x0, waiting for transfers between devices: 45.6 us -> none  [on_device(): lax.all_gather(tokens.astype(jnp.bfloat16), 'tensor', axis=3, tiled=True)]
    all_to_all x0 -> x1, starting transfers between devices: none -> 7.85 us  [on_device(): lax.all_to_all(jnp.stack([tokens.astype(jnp.bfloat16)] * lax.axis_size('t...]
    all_to_all x0 -> x1, local copies, waits for them, and re-layouts: none -> 3.91 us  [on_device(): lax.all_to_all(jnp.stack([tokens.astype(jnp.bfloat16)] * lax.axis_size('t...]
  transfers between devices with their start and end apart: 6 -> 6, of which waited for: 6 -> 6; matrix products, arithmetic and copies ran while one was open for 9% -> 7% of each run, Pallas kernels for 0% -> 0%
where the time goes in v1:
time: 235 us; the launch traced here: 234 us
  waiting for transfers between devices  131 us (56%)
  starting transfers between devices  45.1 us (19%)
  local copies, waits for them, and re-layouts  18.6 us (8%)
  matrix products  14.9 us (6%)
  between operations  13.7 us (6%)
  other arithmetic  10.5 us (4%)
    reduce_scatter x1, waiting for transfers between devices, on_device(): lax.psum_scatter(partial_out, 'tensor', scatter_dimension=3, tiled=True)  61.4 us
    all_to_all x1, waiting for transfers between devices, on_device(): lax.all_to_all(jnp.stack([tokens.astype(jnp.bfloat16)] * lax.axis_size('t...  49.1 us
    all_to_all x1, starting transfers between devices, on_device(): lax.all_to_all(logdecay, 'space', split_axis=2, concat_axis=1, tiled=True)  13.3 us
    all_to_all x1, starting transfers between devices, on_device(): lax.all_to_all(column_out, 'space', split_axis=1, concat_axis=2, tiled=True)  10.1 us
    all_to_all x1, starting transfers between devices, on_device(): lax.all_to_all(value, 'space', split_axis=2, concat_axis=1, tiled=True)  7.85 us
    all_to_all x1, starting transfers between devices, on_device(): lax.all_to_all(jnp.stack([tokens.astype(jnp.bfloat16)] * lax.axis_size('t...  7.85 us
    all_to_all x1, waiting for transfers between devices, on_device(): lax.all_to_all(column_out, 'space', split_axis=1, concat_axis=2, tiled=True)  6.31 us
    all_to_all x1, waiting for transfers between devices, on_device(): lax.all_to_all(value, 'space', split_axis=2, concat_axis=1, tiled=True)  6.09 us
  transfers between devices with their start and end apart: 6, of which 6 were waited for; matrix products, arithmetic and copies ran while one was open for 7% of the time, Pallas kernels for 0%

profile of v1, /device:TPU:19, one launch (start us, length us, event | category | flops | bytes accessed | tf_op | source)
XLA Modules:
  0.0 234.2 jit_solution(297010515777903410)
XLA Ops:
  6.5 1.2 convert_element_type.86
  7.7 1.6 stack.2
  9.3 7.8 %all-to-all-start = ((bf16[8,2,2,128,256]{4,3,2,1,0:T(8,128)(2,1)}), bf16[8,2,2,128,256]{4,3,2,1,0:T(8,128)(2,1)}, u32[]{:S(2)}, u32[]{:S(2)}) async-start(bf16[8,2,2,128,256]{4,3,2,1,0:T(8,128)(2,1)} %stack.2), calls=%async_computation | async-start | bytes 4194304 | tf_op jit(solution)/shard_map/all_to_all | solution.py:53
  17.2 49.1 %all-to-all-done = bf16[8,2,2,128,256]{4,3,2,1,0:T(8,128)(2,1)} async-done(((bf16[8,2,2,128,256]{4,3,2,1,0:T(8,128)(2,1)}), bf16[8,2,2,128,256]{4,3,2,1,0:T(8,128)(2,1)}, u32[]{:S(2)}, u32[]{:S(2)}) %all-to-all-start) | async-done | bytes 2097184 | tf_op jit(solution)/shard_map/all_to_all | solution.py:53
  66.2 3.9 %copy.65 = bf16[8,2,2,128,256]{3,4,0,2,1:T(8,128)(2,1)} copy(bf16[8,2,2,128,256]{4,3,2,1,0:T(8,128)(2,1)} %all-to-all-done) | data formatting | bytes 4194304 | tf_op jit(solution)/shard_map/all_to_all | solution.py:53
  70.1 2.2 multiply_reduce_fusion
  72.4 0.6 fusion.1
  73.0 1.3 copy-done.1
  74.3 0.4 multiply_convert_fusion.7
  74.7 0.8 copy.77
  75.6 13.3 %all-to-all-start.3 = ((bf16[2,2,128,6]{3,1,0,2:T(2,128)(2,1)}), bf16[2,2,128,6]{3,1,0,2:T(2,128)(2,1)S(1)}, u32[]{:S(2)}, u32[]{:S(2)}) async-start(bf16[2,2,128,6]{3,1,0,2:T(2,128)(2,1)} %copy.77), calls=%async_computation.3 | async-start | bytes 262144 | tf_op jit(solution)/shard_map/all_to_all | solution.py:80
  88.9 2.4 %convolution_convert_fusion.1 = bf16[2,2,128,256]{3,2,1,0:T(8,128)(2,1)S(1)} fusion(bf16[2,2,128,2048]{2,3,1,0:T(8,128)(2,1)} %copy-done.1, bf16[2048,256]{1,0:T(8,128)(2,1)S(1)} %copy-done.4), kind=kOutput, calls=%fused_computation.13 | convolution fusion | flops 537001984 | bytes 3407872 | tf_op jit(solution)/shard_map/irwd,dc->irwc/dot_general | solution.py:64
  91.3 1.0 copy.73
  92.2 5.6 %all-to-all-done.3 = bf16[2,2,128,6]{3,1,0,2:T(2,128)(2,1)S(1)} async-done(((bf16[2,2,128,6]{3,1,0,2:T(2,128)(2,1)}), bf16[2,2,128,6]{3,1,0,2:T(2,128)(2,1)S(1)}, u32[]{:S(2)}, u32[]{:S(2)}) %all-to-all-start.3) | async-done | bytes 6176 | tf_op jit(solution)/shard_map/all_to_all | solution.py:80
  97.8 6.0 %all-to-all-start.2 = ((bf16[2,2,128,256]{3,1,0,2:T(2,128)(2,1)}), bf16[2,2,128,256]{3,1,0,2:T(2,128)(2,1)}, u32[]{:S(2)}, u32[]{:S(2)}) async-start(bf16[2,2,128,256]{3,1,0,2:T(2,128)(2,1)} %copy.73), calls=%async_computation.2 | async-start | bytes 524288 | tf_op jit(solution)/shard_map/all_to_all | solution.py:79
  103.9 0.7 mul.108
  104.6 0.3 copy.68
  104.9 4.2 %multiply_convert_fusion.5 = (bf16[2,2,128,384]{3,2,1,0:T(8,128)(2,1)S(1)}, f32[2,2,128,384]{3,2,1,0:T(8,128)}) fusion(f32[2,2,128,384]{3,2,1,0:T(8,128)S(1)} %copy.68, bf16[2,2,128,2048]{2,3,1,0:T(8,128)(2,1)} %copy-done.1, bf16[2048,384]{1,0:T(8,128)(2,1)} %param.12), kind=kOutput, calls=%fused_computation.33 | convolution fusion | flops 806092800 | bytes 5636096 | tf_op jit(solution)/shard_map/irwd,dc->irwc/dot_general | solution.py:61
  109.1 1.1 copy.71
  110.3 3.0 %all-to-all-done.2 = bf16[2,2,128,256]{3,1,0,2:T(2,128)(2,1)} async-done(((bf16[2,2,128,256]{3,1,0,2:T(2,128)(2,1)}), bf16[2,2,128,256]{3,1,0,2:T(2,128)(2,1)}, u32[]{:S(2)}, u32[]{:S(2)}) %all-to-all-start.2) | async-done | bytes 262176 | tf_op jit(solution)/shard_map/all_to_all | solution.py:79
  113.3 7.8 %all-to-all-start.1 = ((bf16[2,2,128,384]{3,1,0,2:T(2,128)(2,1)}), bf16[2,2,128,384]{3,1,0,2:T(2,128)(2,1)S(1)}, u32[]{:S(2)}, u32[]{:S(2)}) async-start(bf16[2,2,128,384]{3,1,0,2:T(2,128)(2,1)} %copy.71), calls=%async_computation.1 | async-start | bytes 786432 | tf_op jit(solution)/shard_map/all_to_all | solution.py:78
  121.1 0.6 iota_compare_fusion
  121.8 0.2 copy.79
  122.0 0.2 copy.80
  122.2 0.1 copy.81
  122.3 1.1 reduce_window_sum.18
  123.5 1.2 copy.74
  124.7 0.2 fusion.49
  124.9 0.2 fusion.36
  125.1 6.1 %all-to-all-done.1 = bf16[2,2,128,384]{3,1,0,2:T(2,128)(2,1)S(1)} async-done(((bf16[2,2,128,384]{3,1,0,2:T(2,128)(2,1)}), bf16[2,2,128,384]{3,1,0,2:T(2,128)(2,1)S(1)}, u32[]{:S(2)}, u32[]{:S(2)}) %all-to-all-start.1) | async-done | bytes 393248 | tf_op jit(solution)/shard_map/all_to_all | solution.py:78
  131.2 0.3 copy.105
  131.5 1.6 reshape.73
  133.0 2.5 %convolution_convert_fusion = bf16[2,2,6,64,128]{4,3,2,1,0:T(8,128)(2,1)S(1)} fusion(bf16[2,128,2,6,64]{4,3,2,1,0:T(8,128)(2,1)} %reshape.73, f32[2,2,6,128]{3,2,1,0:T(8,128)S(1)} %bitcast_subtract_fusion, f32[2,2,6,128]{3,2,1,0:T(8,128)S(1)} %reduce_window_sum.18, f32[2,2,128,128]{3,2,1,0:T(8,128)S(1)} %fusion.36, pred[128,128]{1,0:T(8,128)(4,1)S(1)} %copy-done.6, ...), kind=kOutput, calls=%fused_computation.12 | convolution fusion | flops 53280768 | bytes 1105920 | tf_op jit(solution)/shard_map/iahlm,imahp->ilahp/dot_general | solution.py:43
  135.5 1.1 copy.83
  136.6 10.1 %all-to-all-start.4 = ((bf16[2,128,2,384]{3,2,0,1:T(2,128)(2,1)}), bf16[2,128,2,384]{3,2,0,1:T(2,128)(2,1)S(1)}, u32[]{:S(2)}, u32[]{:S(2)}) async-start(bf16[2,128,2,384]{3,2,0,1:T(2,128)(2,1)} %copy.83), calls=%async_computation.4 | async-start | bytes 786432 | tf_op jit(solution)/shard_map/all_to_all | solution.py:82
  146.8 0.2 copy.69
  147.1 1.2 reduce_window_sum.17
  148.3 0.2 fusion.33
  148.5 1.8 fusion.13
  150.3 0.3 copy.87
  150.6 6.3 %all-to-all-done.4 = bf16[2,128,2,384]{3,2,0,1:T(2,128)(2,1)S(1)} async-done(((bf16[2,128,2,384]{3,2,0,1:T(2,128)(2,1)}), bf16[2,128,2,384]{3,2,0,1:T(2,128)(2,1)S(1)}, u32[]{:S(2)}, u32[]{:S(2)}) %all-to-all-start.4) | async-done | bytes 393248 | tf_op jit(solution)/shard_map/all_to_all | solution.py:82
  156.9 0.6 copy.85
  157.6 0.3 copy.86
  157.8 1.4 reshape.75
  159.3 1.6 multiply_reduce_fusion.1
  160.9 3.3 %fusion.2 = f32[2,2,128,2048]{3,2,1,0:T(8,128)} fusion(bf16[384,2048]{1,0:T(8,128)(2,1)S(1)} %copy-done, f32[2,2,128,384]{3,2,1,0:T(8,128)S(1)} %get-tuple-element.6, f32[384]{0:T(512)S(1)} %copy-done.12, f32[2,2,128]{2,1,0:T(2,128)S(1)} %add_rsqrt_fusion), kind=kOutput, calls=%fused_computation.4 | convolution fusion | flops 805896192 | bytes 6557184 | tf_op jit(solution)/shard_map/irwc,cd->irwd/dot_general | solution.py:90
  164.2 61.4 %reduce-scatter.2.cloned.1.call-done = f32[2,2,128,256]{3,2,1,0:T(8,128)} async-done(((f32[2,2,128,2048]{3,2,1,0:T(8,128)}), f32[2,2,128,256]{3,2,1,0:T(8,128)}) %reduce-scatter.2.cloned.1.call-update) | async-done | bytes 524304 | tf_op jit(solution)/shard_map/reduce_scatter | solution.py:91
  225.6 1.8 add_convert_fusion
  (43 shorter events, 0.6 us)
Async XLA Ops:
  6.5 154.3 %copy-start = (bf16[384,2048]{1,0:T(8,128)(2,1)S(1)}, bf16[384,2048]{1,0:T(8,128)(2,1)}, u32[]{:S(2)}) copy-start(bf16[384,2048]{1,0:T(8,128)(2,1)} %param.19) | copy-start | bytes 4718596
  9.3 7.8 %copy-start.15 = (f32[6]{0:T(128)S(1)}, f32[6]{0:T(128)}, u32[]{:S(2)}) copy-start(f32[6]{0:T(128)} %param.16) | copy-start | bytes 76
  9.3 56.9 %all-to-all-start = ((bf16[8,2,2,128,256]{4,3,2,1,0:T(8,128)(2,1)}), bf16[8,2,2,128,256]{4,3,2,1,0:T(8,128)(2,1)}, u32[]{:S(2)}, u32[]{:S(2)}) async-start(bf16[8,2,2,128,256]{4,3,2,1,0:T(8,128)(2,1)} %stack.2), calls=%async_computation | async-start | bytes 4194304 | tf_op jit(solution)/shard_map/all_to_all | solution.py:53
  17.1 55.8 %copy-start.8 = (f32[6]{0:T(128)}, f32[6]{0:T(128)S(1)}, u32[]{:S(2)}) copy-start(f32[6]{0:T(128)S(1)} %neg.11) | copy-start | bytes 76
  66.2 6.1 %copy-start.10 = (f32[2048]{0:T(1024)S(1)}, f32[2048]{0:T(1024)}, u32[]{:S(2)}) copy-start(f32[2048]{0:T(1024)} %param.11) | copy-start | bytes 24580
  70.1 2.2 copy-start.2
  72.4 2.0 copy-start.5
  72.4 2.0 copy-start.13
  73.0 1.3 copy-start.1
  74.3 14.6 %copy-start.4 = (bf16[2048,256]{1,0:T(8,128)(2,1)S(1)}, bf16[2048,256]{1,0:T(8,128)(2,1)}, u32[]{:S(2)}) copy-start(bf16[2048,256]{1,0:T(8,128)(2,1)} %param.13) | copy-start | bytes 3145732
  75.6 22.3 %all-to-all-start.3 = ((bf16[2,2,128,6]{3,1,0,2:T(2,128)(2,1)}), bf16[2,2,128,6]{3,1,0,2:T(2,128)(2,1)S(1)}, u32[]{:S(2)}, u32[]{:S(2)}) async-start(bf16[2,2,128,6]{3,1,0,2:T(2,128)(2,1)} %copy.77), calls=%async_computation.3 | async-start | bytes 262144 | tf_op jit(solution)/shard_map/all_to_all | solution.py:80
  88.9 14.9 %copy-start.14 = (f32[6]{0:T(128)S(1)}, f32[6]{0:T(128)}, u32[]{:S(2)}) copy-start(f32[6]{0:T(128)} %param.17) | copy-start | bytes 76
  97.8 15.4 %all-to-all-start.2 = ((bf16[2,2,128,256]{3,1,0,2:T(2,128)(2,1)}), bf16[2,2,128,256]{3,1,0,2:T(2,128)(2,1)}, u32[]{:S(2)}, u32[]{:S(2)}) async-start(bf16[2,2,128,256]{3,1,0,2:T(2,128)(2,1)} %copy.73), calls=%async_computation.2 | async-start | bytes 524288 | tf_op jit(solution)/shard_map/all_to_all | solution.py:79
  113.3 17.9 %all-to-all-start.1 = ((bf16[2,2,128,384]{3,1,0,2:T(2,128)(2,1)}), bf16[2,2,128,384]{3,1,0,2:T(2,128)(2,1)S(1)}, u32[]{:S(2)}, u32[]{:S(2)}) async-start(bf16[2,2,128,384]{3,1,0,2:T(2,128)(2,1)} %copy.71), calls=%async_computation.1 | async-start | bytes 786432 | tf_op jit(solution)/shard_map/all_to_all | solution.py:78
  124.6 8.4 %copy-start.6 = (pred[128,128]{1,0:T(8,128)(4,1)S(1)}, pred[128,128]{1,0:T(8,128)(4,1)}, u32[]{:S(2)}) copy-start(pred[128,128]{1,0:T(8,128)(4,1)} %get-tuple-element.14) | copy-start | bytes 49156
  124.7 8.4 %copy-start.7 = (pred[128,128]{1,0:T(8,128)(4,1)S(1)}, pred[128,128]{1,0:T(8,128)(4,1)}, u32[]{:S(2)}) copy-start(pred[128,128]{1,0:T(8,128)(4,1)} %get-tuple-element.15) | copy-start | bytes 49156
  135.5 11.3 %copy-start.9 = (f32[6]{0:T(128)S(1)}, f32[6]{0:T(128)}, u32[]{:S(2)}) copy-start(f32[6]{0:T(128)} %copy-done.8) | copy-start | bytes 76
  136.6 20.3 %all-to-all-start.4 = ((bf16[2,128,2,384]{3,2,0,1:T(2,128)(2,1)}), bf16[2,128,2,384]{3,2,0,1:T(2,128)(2,1)S(1)}, u32[]{:S(2)}, u32[]{:S(2)}) async-start(bf16[2,128,2,384]{3,2,0,1:T(2,128)(2,1)} %copy.83), calls=%async_computation.4 | async-start | bytes 786432 | tf_op jit(solution)/shard_map/all_to_all | solution.py:82
  146.7 78.8 %reduce-scatter.2.cloned.1.call-start = ((), (), s32[]{:S(2)}) async-start(), calls=%async_computation.6 | async-start | bytes 4718592 | tf_op jit(solution)/shard_map/reduce_scatter | solution.py:91
  157.6 1.7 copy-start.11
  159.3 1.6 copy-start.12
  164.2 61.4 %copy-start.3 = (f32[2,2,128,256]{3,2,1,0:T(8,128)S(1)}, f32[2,2,128,256]{3,2,1,0:T(8,128)}, u32[]{:S(2)}) copy-start(f32[2,2,128,256]{3,2,1,0:T(8,128)} %param.10) | copy-start | bytes 1572868
Sparse Core Ops, SparseCore 0:
  164.3 61.2 reduce-scatter.1
